TPU v7x, 32 devices: a whole 2x2x4 slice. The times are simulated.
32 devices in a mesh: cluster: 4 (over x, core), leaf: 8 (over z, y).
Axes of the slice: x: 2, y: 2, z: 4, core: 2. Of those that a mesh axis runs over, the one named last changes fastest.
Arguments:
- probes: float32 [32768, 512], P(('cluster', 'leaf')), may hold values from -6 to 6
- dense_leaf: float32 [32768, 1024], P(('cluster', 'leaf')), may hold values from -0.1875 to 0.1875
- leaf_basis: float32 [32768, 128], P(('cluster', 'leaf')), may hold values from -0.1875 to 0.1875
- sibling_cores: float32 [32, 8, 128, 128], P(('cluster', 'leaf')), may hold values from -0.5 to 0.5
- transfer: float32 [32, 128, 128], P(('cluster', 'leaf')), may hold values from -0.5 to 0.5
- cluster_cores: float32 [4, 4, 128, 128], P('cluster'), may hold values from -0.1875 to 0.1875
Outputs:
- product: float32 [32768, 512], P(('cluster', 'leaf'))
All inputs are finite; a program needn't handle non-finite values.
Results may differ from a plain program's by a relative error of at most 0.00005.
Values sent between devices are 32-bit elements; how exact they have to be, the bound alone decides.
No kernel may reach another device: no remote copies, remote signals or barrier semaphores. Data moves between devices by JAX's collectives and lax.ppermute only.
A program may use at most 128 MiB of HBM per device.

v0:
```python
import jax
import jax.numpy as jnp
from jax import lax
from jax.sharding import PartitionSpec as P

HI = lax.Precision.HIGHEST


def local(probes, dense_leaf, leaf_basis, sibling_cores, transfer, cluster_cores):
    own = lax.axis_index("leaf")
    cown = lax.axis_index("cluster")
    cores = sibling_cores[0]
    trans = transfer[0]
    outer_cores = cluster_cores[0]
    rank_two = trans.shape[1]
    near = jnp.dot(dense_leaf, probes, precision=HI) + jnp.dot(dense_leaf.T, probes, precision=HI)
    coef = jnp.dot(leaf_basis.T, probes, precision=HI)
    turned = lax.all_to_all(cores, "leaf", split_axis=0, concat_axis=0, tiled=True)
    used = cores + jnp.transpose(turned, (0, 2, 1))
    piece = lax.all_gather(coef[None], "leaf", axis=0, tiled=True)
    count = piece.shape[0]
    block = used
    keep = (jnp.arange(count, dtype=jnp.int32) != own).astype(jnp.float32)
    block = block * keep[:, None, None]
    sib = jnp.einsum("jab,jbp->ap", block, piece, precision=HI)
    local_g = jnp.dot(trans.T, coef, precision=HI)
    nclu = outer_cores.shape[0]
    bkeep = (jnp.arange(nclu, dtype=jnp.int32) != cown).astype(jnp.float32)[:, None, None]
    masked = outer_cores * bkeep
    g_whole = lax.psum(local_g, "leaf")
    gathered = lax.all_gather(g_whole[None], "cluster", axis=0, tiled=True)
    front = jnp.einsum("dab,dbp->ap", masked, gathered, precision=HI)
    number = rank_two * lax.axis_size("cluster") // rank_two
    block = masked
    terms = jnp.einsum("dba,bp->dap", block, g_whole, precision=HI)
    field = front + lax.psum_scatter(
        terms.reshape(number * rank_two, g_whole.shape[1]),
        "cluster",
        scatter_dimension=0,
        tiled=True,
    )
    total = sib + jnp.dot(trans, field, precision=HI)
    return near + jnp.dot(leaf_basis, total, precision=HI)


def solution(mesh):
    return jax.shard_map(
        local,
        mesh=mesh,
        in_specs=(
            P(("cluster", "leaf"), None),
            P(("cluster", "leaf"), None),
            P(("cluster", "leaf"), None),
            P(("cluster", "leaf"), None, None, None),
            P(("cluster", "leaf"), None, None),
            P("cluster", None, None, None),
        ),
        out_specs=P(("cluster", "leaf"), None),
        check_vma=False,
    )
```

profile of v0, /device:TPU:0, one launch (start us, length us, event | category | flops | bytes accessed | tf_op | source)
XLA Modules:
  0.0 197.5 jit_solution(9313554170039844846)
XLA Ops:
  6.5 0.0 copy-start
  6.5 0.0 copy-start.6
  6.5 0.0 copy-start.5
  6.5 0.0 all-reduce.2.cloned.1.call-start
  6.5 1.6 copy-done
  8.1 2.4 %fusion.10 = f32[128,512]{1,0:T(8,128)S(1)} fusion(f32[1024,128]{1,0:T(8,128)} %param.8, f32[1024,512]{1,0:T(8,128)S(1)} %copy-done), kind=kOutput, calls=%fused_computation.18 | convolution fusion | flops 805306368 | bytes 2883584 | tf_op jit(solution)/shard_map/dot_general | solution.py:17
  10.5 0.0 copy-start.3
  10.6 0.0 copy-done.6
  10.6 1.3 convolution_bitcast_fusion.3
  11.9 0.0 all-reduce.2.cloned.1.call-update
  11.9 0.0 all-gather.7.cloned.1.call-start
  11.9 73.8 %all-reduce.2.cloned.1.call-done = f32[128,512]{0,1:T(8,128)} async-done(((f32[128,512]{0,1:T(8,128)}), f32[128,512]{0,1:T(8,128)}) %all-reduce.2.cloned.1.call-update) | async-done | bytes 262160 | tf_op jit(solution)/shard_map/psum | solution.py:30
  85.8 0.0 copy-start.4
  85.8 0.0 all-gather.7.cloned.1.call-update
  85.8 0.0 reduce-scatter.2.cloned.1.call-start
  85.8 0.0 copy-done.5
  85.8 0.1 copy.10
  86.0 0.1 bitcast_multiply_fusion
  86.1 2.9 %fusion.11 = f32[512,512]{1,0:T(8,128)} fusion(f32[512,128]{1,0:T(8,128)S(1)} %bitcast.52, f32[128,512]{0,1:T(8,128)} %all-reduce.2.cloned.1.call-done), kind=kOutput, calls=%fused_computation.19 | convolution fusion | flops 402653184 | bytes 1572864 | tf_op jit(solution)/shard_map/dba,bp->dap/dot_general | solution.py:35
  89.0 0.0 reduce-scatter.2.cloned.1.call-update
  89.0 0.0 copy-done.3
  89.1 0.0 all-gather.5.cloned.1.call-start
  89.1 0.5 all-gather.5.cloned.1.call-update
  89.6 0.0 copy-done.4
  89.6 1.0 copy.9
  90.6 4.3 %all-to-all-start = ((f32[8,128,128]{1,2,0:T(8,128)}), f32[8,128,128]{1,2,0:T(8,128)}, u32[]{:S(2)}, u32[]{:S(2)}) async-start(f32[8,128,128]{1,2,0:T(8,128)} %copy.9), calls=%async_computation | async-start | bytes 1048576 | tf_op jit(solution)/shard_map/all_to_all | solution.py:18
  95.0 9.6 %fusion.8 = f32[1024,512]{1,0:T(8,128)} fusion(f32[1024,1024]{1,0:T(8,128)} %param.7, f32[1024,512]{1,0:T(8,128)S(1)} %copy-done), kind=kOutput, calls=%fused_computation.16 | convolution fusion | flops 6442450944 | bytes 8388608 | tf_op jit(solution)/shard_map/dot_general | solution.py:16
  104.6 9.6 %fusion.9 = f32[1024,512]{1,0:T(8,128)} fusion(f32[1024,1024]{1,0:T(8,128)} %param.7, f32[1024,512]{1,0:T(8,128)S(1)} %copy-done), kind=kOutput, calls=%fused_computation.17 | convolution fusion | flops 6442450944 | bytes 8388608 | tf_op jit(solution)/shard_map/dot_general | solution.py:16
  114.2 0.0 all-gather.7.cloned.1.call-done
  114.2 1.6 copy.14
  115.8 15.0 %reduce-scatter.2.cloned.1.call-done = f32[128,512]{1,0:T(8,128)} async-done(((f32[512,512]{1,0:T(8,128)}), f32[128,512]{1,0:T(8,128)}) %reduce-scatter.2.cloned.1.call-update) | async-done | bytes 262160 | tf_op jit(solution)/shard_map/reduce_scatter | solution.py:36
  130.7 2.4 %fusion.1 = f32[128,512]{1,0:T(8,128)} fusion(f32[128,512]{1,0:T(8,128)} %reduce-scatter.2.cloned.1.call-done, f32[4,128,128]{1,2,0:T(8,128)S(1)} %bitcast_multiply_fusion, f32[4,128,512]{2,1,0:T(8,128)S(1)} %bitcast.51), kind=kOutput, calls=%fused_computation.6 | convolution fusion | flops 402718720 | bytes 1835008 | tf_op jit(solution)/shard_map/dab,dbp->ap/dot_general | solution.py:32
  133.1 0.0 all-to-all-done
  133.1 48.7 %all-gather.5.cloned.1.call-done = f32[1024,512]{1,0:T(8,128)} async-done(((f32[128,512]{1,0:T(8,128)}), f32[1024,512]{1,0:T(8,128)}) %all-gather.5.cloned.1.call-update) | async-done | bytes 2097168 | tf_op jit(solution)/shard_map/all_gather | solution.py:20
  181.8 0.0 copy-start.1
  181.8 0.0 copy-start.2
  181.8 3.4 %convolution_bitcast_fusion = f32[128,512]{1,0:T(8,128)S(1)} fusion(f32[8,128,512]{2,1,0:T(8,128)} %bitcast.53, f32[8,128,128]{1,2,0:T(8,128)} %all-to-all-done, f32[8]{0:T(128)S(1)} %compare_convert_fusion.1, f32[1,8,128,128]{3,2,1,0:T(8,128)} %param.9), kind=kOutput, calls=%fused_computation.1 | convolution fusion | flops 805568512 | bytes 3407904 | tf_op jit(solution)/shard_map/jab,jbp->ap/dot_general | solution.py:25
  185.2 1.3 fusion
  186.5 0.0 copy-done.1
  186.6 0.0 copy-done.2
  186.6 4.4 %bitcast_add_fusion = f32[1024,512]{1,0:T(8,128)} fusion(f32[1024,512]{1,0:T(8,128)S(1)} %copy-done.2, f32[1024,512]{1,0:T(8,128)S(1)} %copy-done.1, f32[128,512]{1,0:T(8,128)S(1)} %fusion, f32[1024,128]{1,0:T(8,128)} %param.8), kind=kOutput, calls=%fused_computation | convolution fusion | flops 806354944 | bytes 7077888 | tf_op jit(solution)/shard_map/dot_general | solution.py:43
  (2 shorter events, 0.0 us)
Async XLA Ops:
  6.5 1.6 copy-start
  6.5 4.0 %copy-start.6 = (f32[1,128,128]{2,1,0:T(8,128)S(1)}, f32[1,128,128]{2,1,0:T(8,128)}, u32[]{:S(2)}) copy-start(f32[1,128,128]{2,1,0:T(8,128)} %param.10) | copy-start | bytes 196612
  6.5 79.3 %copy-start.5 = (f32[1,4,128,128]{3,2,1,0:T(8,128)S(1)}, f32[1,4,128,128]{3,2,1,0:T(8,128)}, u32[]{:S(2)}) copy-start(f32[1,4,128,128]{3,2,1,0:T(8,128)} %param.11) | copy-start | bytes 786436
  6.5 79.2 %all-reduce.2.cloned.1.call-start = ((), (), s32[]{:S(2)}) async-start(), calls=%async_computation.2 | async-start | bytes 524288 | tf_op jit(solution)/shard_map/psum | solution.py:30
  10.5 78.5 %copy-start.3 = (f32[128,512]{1,0:T(8,128)}, f32[128,512]{1,0:T(8,128)S(1)}, u32[]{:S(2)}) copy-start(f32[128,512]{1,0:T(8,128)S(1)} %fusion.10) | copy-start | bytes 786436
  11.9 102.3 %all-gather.7.cloned.1.call-start = ((), (), s32[]{:S(2)}) async-start(), calls=%async_computation.5 | async-start | bytes 1310720 | tf_op jit(solution)/shard_map/all_gather | solution.py:31
  85.8 3.9 %copy-start.4 = (f32[1,8,128,128]{3,2,1,0:T(8,128)S(1)}, f32[1,8,128,128]{3,2,1,0:T(8,128)}, u32[]{:S(2)}) copy-start(f32[1,8,128,128]{3,2,1,0:T(8,128)} %param.9) | copy-start | bytes 1572868
  85.8 44.9 %reduce-scatter.2.cloned.1.call-start = ((), (), s32[]{:S(2)}) async-start(), calls=%async_computation.3 | async-start | bytes 1310720 | tf_op jit(solution)/shard_map/reduce_scatter | solution.py:36
  89.1 92.8 %all-gather.5.cloned.1.call-start = ((), (), s32[]{:S(2)}) async-start(), calls=%async_computation.4 | async-start | bytes 2359296 | tf_op jit(solution)/shard_map/all_gather | solution.py:20
  90.6 42.5 %all-to-all-start = ((f32[8,128,128]{1,2,0:T(8,128)}), f32[8,128,128]{1,2,0:T(8,128)}, u32[]{:S(2)}, u32[]{:S(2)}) async-start(f32[8,128,128]{1,2,0:T(8,128)} %copy.9), calls=%async_computation | async-start | bytes 1048576 | tf_op jit(solution)/shard_map/all_to_all | solution.py:18
  181.8 4.7 %copy-start.1 = (f32[1024,512]{1,0:T(8,128)S(1)}, f32[1024,512]{1,0:T(8,128)}, u32[]{:S(2)}) copy-start(f32[1024,512]{1,0:T(8,128)} %fusion.9) | copy-start | bytes 6291460
  181.8 4.7 %copy-start.2 = (f32[1024,512]{1,0:T(8,128)S(1)}, f32[1024,512]{1,0:T(8,128)}, u32[]{:S(2)}) copy-start(f32[1024,512]{1,0:T(8,128)} %fusion.8) | copy-start | bytes 6291460
Sparse Core Ops, SparseCore 0:
  12.0 73.7 all-reduce.1
  87.3 16.0 all-gather.6
  105.9 24.7 reduce-scatter.1
  132.7 49.0 all-gather.4
where the time goes:
time: 198 us; the launch traced here: 197 us
  waiting for transfers between devices  138 us (70%)
  matrix products  37.3 us (19%)
  between operations  13.3 us (7%)
  starting transfers between devices  4.44 us (2%)
  local copies, waits for them, and re-layouts  4.31 us (2%)
    psum x1, waiting for transfers between devices, local(): g_whole = lax.psum(local_g, 'leaf')  73.8 us
    all_gather x1, waiting for transfers between devices, local(): piece = lax.all_gather(coef[None], 'leaf', axis=0, tiled=True)  48.7 us
    reduce_scatter x1, waiting for transfers between devices, local(): lax.psum_scatter(terms.reshape(number * rank_two, g_whole.shape[1]), 'clu...  15 us
    dot_general x1, matrix products, local(): jnp.dot(dense_leaf.T, probes, precision=HI)  9.6 us
    dot_general x1, matrix products, local(): jnp.dot(dense_leaf, probes, precision=HI)  9.59 us
    dot_general x1, matrix products, local(): return near + jnp.dot(leaf_basis, total, precision=HI)  4.38 us
    all_to_all x1, starting transfers between devices, local(): lax.all_to_all(cores, 'leaf', split_axis=0, concat_axis=0, tiled=True)  4.32 us
  transfers between devices with their start and end apart: 5, of which 3 were waited for; matrix products, arithmetic and copies ran while one was open for 14% of the time, Pallas kernels for 0%

commit v1 on v0

--- a/solution.py
+++ b/solution.py
@@ -17,7 +17,12 @@
     coef = jnp.dot(leaf_basis.T, probes, precision=HI)
     turned = lax.all_to_all(cores, "leaf", split_axis=0, concat_axis=0, tiled=True)
     used = cores + jnp.transpose(turned, (0, 2, 1))
-    piece = lax.all_gather(coef[None], "leaf", axis=0, tiled=True)
+    ring = [coef[None]]
+    for hop in range(7):
+        ring.append(lax.ppermute(ring[-1], "leaf", [(dev, (dev + 1) % 8) for dev in range(8)]))
+    piece = jnp.roll(
+        jnp.concatenate(ring[::-1], axis=0), (lax.axis_index("leaf") + 1) * ring[0].shape[0], axis=0
+    )
     count = piece.shape[0]
     block = used
     keep = (jnp.arange(count, dtype=jnp.int32) != own).astype(jnp.float32)

time: 198 us -> 177 us (0.89)
  waiting for transfers between devices: 138 us -> 89.8 us
  local copies, waits for them, and re-layouts: 4.31 us -> 24.5 us
  starting transfers between devices: 4.44 us -> 12.9 us
    all_gather x1 -> x0, waiting for transfers between devices: 48.7 us -> none  [local(): piece = lax.all_gather(coef[None], 'leaf', axis=0, tiled=True)]
    ppermute x0 -> x7, waiting for transfers between devices: none -> 30.4 us  [local(): lax.ppermute(ring[-1], 'leaf', [(dev, (dev + 1) % 8) for dev in range(8)])]
    unnamed x15 -> x34, local copies, waits for them, and re-layouts: 1.73 us -> 20.1 us
    psum x1, waiting for transfers between devices: 73.8 us -> 59.1 us  [local(): g_whole = lax.psum(local_g, 'leaf')]
    reduce_scatter x1, waiting for transfers between devices: 15 us -> 0.2 us  [local(): lax.psum_scatter(terms.reshape(number * rank_two, g_whole.shape[1]), 'clu...]
    ppermute x0 -> x7, starting transfers between devices: none -> 6.78 us  [local(): lax.ppermute(ring[-1], 'leaf', [(dev, (dev + 1) % 8) for dev in range(8)])]
  transfers between devices with their start and end apart: 5 -> 11, of which waited for: 3 -> 6; matrix products, arithmetic and copies ran while one was open for 14% -> 27% of each run, Pallas kernels for 0% -> 0%
where the time goes in v1:
time: 177 us
  waiting for transfers between devices  89.8 us (51%)
  matrix products  36.1 us (20%)
  local copies, waits for them, and re-layouts  24.5 us (14%)
  between operations  13.3 us (8%)
  starting transfers between devices  12.9 us (7%)
    psum x1, waiting for transfers between devices, local(): g_whole = lax.psum(local_g, 'leaf')  59.1 us
    ppermute x7, waiting for transfers between devices, local(): lax.ppermute(ring[-1], 'leaf', [(dev, (dev + 1) % 8) for dev in range(8)])  30.4 us
    unnamed x34, local copies, waits for them, and re-layouts  20.1 us
    dot_general x1, matrix products, local(): jnp.dot(dense_leaf, probes, precision=HI)  9.94 us
    dot_general x1, matrix products, local(): jnp.dot(dense_leaf.T, probes, precision=HI)  8.14 us
    ppermute x7, starting transfers between devices, local(): lax.ppermute(ring[-1], 'leaf', [(dev, (dev + 1) % 8) for dev in range(8)])  6.78 us
    all_to_all x1, starting transfers between devices, local(): lax.all_to_all(cores, 'leaf', split_axis=0, concat_axis=0, tiled=True)  6 us
    dot_general x1, matrix products, local(): return near + jnp.dot(leaf_basis, total, precision=HI)  4.89 us
  transfers between devices with their start and end apart: 11, of which 6 were waited for; matrix products, arithmetic and copies ran while one was open for 27% of the time, Pallas kernels for 0%

profile of v1, /device:TPU:0, one launch (start us, length us, event | category | flops | bytes accessed | tf_op | source)
XLA Modules:
  0.0 176.6 jit_solution(17873722249513715591)
XLA Ops:
  6.5 0.0 copy-start
  6.5 0.0 all-reduce.2.cloned.1.call-start
  6.5 1.6 copy-done
  8.1 2.4 %fusion.18 = f32[128,512]{1,0:T(8,128)S(1)} fusion(f32[1024,128]{1,0:T(8,128)} %param.8, f32[1024,512]{1,0:T(8,128)S(1)} %copy-done), kind=kOutput, calls=%fused_computation.37 | convolution fusion | flops 805306368 | bytes 2883584 | tf_op jit(solution)/shard_map/dot_general | solution.py:17
  10.5 3.0 %collective-permute-start = (f32[1,128,512]{2,1,0:T(8,128)S(1)}, f32[1,128,512]{2,1,0:T(8,128)S(1)}, u32[]{:S(2)}, u32[]{:S(2)}) collective-permute-start(f32[1,128,512]{2,1,0:T(8,128)S(1)} %bitcast.53), channel_id=1, source_target_pairs={{0,1},{1,2},{2,3},{3,4},{4,5},{5,6},{6,7},{7,0},{8,9},{9,10},{10,1... | collective-permute-start | bytes 786440 | tf_op jit(solution)/shard_map/ppermute | solution.py:22
  13.6 9.3 %collective-permute-done = f32[1,128,512]{2,1,0:T(8,128)S(1)} collective-permute-done((f32[1,128,512]{2,1,0:T(8,128)S(1)}, f32[1,128,512]{2,1,0:T(8,128)S(1)}, u32[]{:S(2)}, u32[]{:S(2)}) %collective-permute-start) | collective-permute-done | bytes 262176 | tf_op jit(solution)/shard_map/ppermute | solution.py:22
  22.9 0.0 collective-permute-start.1
  22.9 2.2 %convolution_bitcast_fusion.2 = f32[128,512]{0,1:T(8,128)} fusion(f32[128,512]{1,0:T(8,128)S(1)} %fusion.18, f32[1,128,128]{2,1,0:T(8,128)} %param.10), kind=kOutput, calls=%fused_computation.6 | convolution fusion | flops 100663296 | bytes 589824 | tf_op jit(solution)/shard_map/dot_general | solution.py:31
  25.1 0.0 all-reduce.2.cloned.1.call-update
  25.1 8.0 %collective-permute-done.1 = f32[1,128,512]{2,1,0:T(8,128)S(1)} collective-permute-done((f32[1,128,512]{2,1,0:T(8,128)S(1)}, f32[1,128,512]{2,1,0:T(8,128)S(1)}, u32[]{:S(2)}, u32[]{:S(2)}) %collective-permute-start.1) | collective-permute-done | bytes 262176 | tf_op jit(solution)/shard_map/ppermute | solution.py:22
  33.1 0.0 collective-permute-start.2
  33.1 2.1 %copy.9 = f32[8,128,128]{1,2,0:T(8,128)} copy(f32[8,128,128]{2,1,0:T(8,128)} %bitcast.55) | data formatting | bytes 1048576 | tf_op jit(solution)/shard_map/squeeze | solution.py:12
  35.2 6.0 %all-to-all-start = ((f32[8,128,128]{1,2,0:T(8,128)}), f32[8,128,128]{1,2,0:T(8,128)}, u32[]{:S(2)}, u32[]{:S(2)}) async-start(f32[8,128,128]{1,2,0:T(8,128)} %copy.9), calls=%async_computation | async-start | bytes 1048576 | tf_op jit(solution)/shard_map/all_to_all | solution.py:18
  41.2 0.0 all-gather.3.cloned.1.call-start
  41.2 59.1 %all-reduce.2.cloned.1.call-done = f32[128,512]{0,1:T(8,128)} async-done(((f32[128,512]{0,1:T(8,128)}), f32[128,512]{0,1:T(8,128)}) %all-reduce.2.cloned.1.call-update) | async-done | bytes 262160 | tf_op jit(solution)/shard_map/psum | solution.py:35
  100.3 0.0 all-gather.3.cloned.1.call-update
  100.3 0.0 reduce-scatter.2.cloned.1.call-start
  100.3 0.0 copy-start.1
  100.4 0.0 collective-permute-done.2
  100.4 0.7 collective-permute-start.3
  101.1 9.9 %fusion.16 = f32[1024,512]{1,0:T(8,128)} fusion(f32[1024,1024]{1,0:T(8,128)} %param.7, f32[1024,512]{1,0:T(8,128)S(1)} %copy-done), kind=kOutput, calls=%fused_computation.35 | convolution fusion | flops 6442450944 | bytes 8388608 | tf_op jit(solution)/shard_map/dot_general | solution.py:16
  111.0 0.0 collective-permute-done.3
  111.0 1.5 collective-permute-start.4
  112.6 0.0 copy-done.1
  112.6 8.1 %fusion.17 = f32[1024,512]{1,0:T(8,128)} fusion(f32[1024,1024]{1,0:T(8,128)S(1)} %copy-done.1, f32[1024,512]{1,0:T(8,128)S(1)} %copy-done), kind=kOutput, calls=%fused_computation.36 | convolution fusion | flops 6442450944 | bytes 8388608 | tf_op jit(solution)/shard_map/dot_general | solution.py:16
  120.7 0.0 copy-done.6
  120.7 0.0 collective-permute-done.4
  120.7 1.5 collective-permute-start.5
  122.2 1.1 copy.10
  123.3 0.1 bitcast_multiply_fusion
  123.4 0.0 copy-start.3
  123.4 0.0 copy-start.7
  123.4 6.8 %collective-permute-done.5 = f32[1,128,512]{2,1,0:T(8,128)} collective-permute-done((f32[1,128,512]{2,1,0:T(8,128)}, f32[1,128,512]{2,1,0:T(8,128)}, u32[]{:S(2)}, u32[]{:S(2)}) %collective-permute-start.5) | collective-permute-done | bytes 262176 | tf_op jit(solution)/shard_map/ppermute | solution.py:22
  130.2 0.0 collective-permute-start.6
  130.2 0.0 copy-done.3
  130.2 3.0 %fusion.19 = f32[512,512]{1,0:T(8,128)} fusion(f32[512,128]{1,0:T(8,128)S(1)} %bitcast.54, f32[128,512]{0,1:T(8,128)} %all-reduce.2.cloned.1.call-done), kind=kOutput, calls=%fused_computation.38 | convolution fusion | flops 402653184 | bytes 1572864 | tf_op jit(solution)/shard_map/dba,bp->dap/dot_general | solution.py:40
  133.2 0.0 reduce-scatter.2.cloned.1.call-update
  133.2 6.4 %collective-permute-done.6 = f32[1,128,512]{2,1,0:T(8,128)} collective-permute-done((f32[1,128,512]{2,1,0:T(8,128)}, f32[1,128,512]{2,1,0:T(8,128)}, u32[]{:S(2)}, u32[]{:S(2)}) %collective-permute-start.6) | collective-permute-done | bytes 262176 | tf_op jit(solution)/shard_map/ppermute | solution.py:22
  139.6 1.7 constant_dynamic-update-slice_fusion.15
  141.2 1.7 constant_dynamic-update-slice_fusion.14
  142.9 1.7 constant_dynamic-update-slice_fusion.13
  144.6 0.0 copy-done.7
  144.6 0.7 constant_dynamic-update-slice_fusion.12
  145.3 0.7 constant_dynamic-update-slice_fusion.11
  146.0 0.7 constant_dynamic-update-slice_fusion.10
  146.7 0.7 constant_dynamic-update-slice_fusion.9
  147.4 0.7 constant_dynamic-update-slice_fusion.8
  148.2 1.7 constant_dynamic-update-slice_fusion.7
  149.9 1.7 constant_dynamic-update-slice_fusion.6
  151.5 1.7 constant_dynamic-update-slice_fusion.5
  153.2 0.7 constant_dynamic-update-slice_fusion.4
  153.9 0.7 constant_dynamic-update-slice_fusion.3
  154.6 0.7 constant_dynamic-update-slice_fusion.2
  155.4 1.6 copy.14
  156.9 1.7 constant_dynamic-update-slice_fusion.1
  158.6 0.7 constant_dynamic-update-slice_fusion
  159.3 0.2 reduce-scatter.2.cloned.1.call-done
  159.5 1.8 %fusion.8 = f32[128,512]{1,0:T(8,128)S(1)} fusion(f32[128,512]{1,0:T(8,128)} %reduce-scatter.2.cloned.1.call-done, f32[4,128,128]{1,2,0:T(8,128)} %copy-done.3, f32[4,128,512]{2,1,0:T(8,128)S(1)} %bitcast.52), kind=kOutput, calls=%fused_computation.8 | convolution fusion | flops 402718720 | bytes 1835008 | tf_op jit(solution)/shard_map/dab,dbp->ap/dot_general | solution.py:37
  161.3 0.0 copy-done.8
  161.3 0.0 copy-start.4
  161.3 0.4 convolution_bitcast_fusion
  161.7 0.0 all-to-all-done
  161.7 3.4 %fusion.5 = f32[128,512]{1,0:T(8,128)S(1)} fusion(f32[128,512]{1,0:T(8,128)S(1)} %convolution_bitcast_fusion, f32[16,128,512]{2,1,0:T(8,128)} %constant_dynamic-update-slice_fusion, s32[]{:T(128)S(6)} %select_n.14, f32[8,128,128]{1,2,0:T(8,128)} %all-to-all-done, f32[8]{0:T(128)S(1)} %compare_convert_fusion.1, f32[1,8,128,128]{3,2,1,0:T(8,128)} %param.9), kind=kOutput, calls=%fused_computation.7 | convolution fusion | flops 805634048 | bytes 3670052 | tf_op jit(solution)/shard_map/jab,jbp->ap/dot_general | solution.py:30
  165.2 4.9 %bitcast_add_fusion = f32[1024,512]{1,0:T(8,128)} fusion(f32[1024,512]{1,0:T(8,128)} %fusion.16, f32[1024,512]{1,0:T(8,128)S(1)} %copy-done.2, f32[128,512]{1,0:T(8,128)S(1)} %fusion.5, f32[1024,128]{1,0:T(8,128)S(1)} %copy-done.4), kind=kOutput, calls=%fused_computation | convolution fusion | flops 806354944 | bytes 7077888 | tf_op jit(solution)/shard_map/dot_general | solution.py:48
  (10 shorter events, 0.0 us)
Async XLA Ops:
  6.5 1.6 copy-start
  6.5 93.7 %all-reduce.2.cloned.1.call-start = ((), (), s32[]{:S(2)}) async-start(), calls=%async_computation.2 | async-start | bytes 524288 | tf_op jit(solution)/shard_map/psum | solution.py:35
  10.5 12.4 %collective-permute-start = (f32[1,128,512]{2,1,0:T(8,128)S(1)}, f32[1,128,512]{2,1,0:T(8,128)S(1)}, u32[]{:S(2)}, u32[]{:S(2)}) collective-permute-start(f32[1,128,512]{2,1,0:T(8,128)S(1)} %bitcast.53), channel_id=1, source_target_pairs={{0,1},{1,2},{2,3},{3,4},{4,5},{5,6},{6,7},{7,0},{8,9},{9,10},{10,1... | collective-permute-start | bytes 786440 | tf_op jit(solution)/shard_map/ppermute | solution.py:22
  22.9 123.8 %copy-start.5 = (f32[1,128,512]{2,1,0:T(8,128)}, f32[1,128,512]{2,1,0:T(8,128)S(1)}, u32[]{:S(2)}) copy-start(f32[1,128,512]{2,1,0:T(8,128)S(1)} %collective-permute-done) | copy-start | bytes 786436
  22.9 10.2 %collective-permute-start.1 = (f32[1,128,512]{2,1,0:T(8,128)S(1)}, f32[1,128,512]{2,1,0:T(8,128)S(1)}, u32[]{:S(2)}, u32[]{:S(2)}) collective-permute-start(f32[1,128,512]{2,1,0:T(8,128)S(1)} %collective-permute-done), channel_id=1, source_target_pairs={{0,1},{1,2},{2,3},{3,4},{4,5},{5,6},{6,7},{7,0},{8,9},{9,10},{10,1... | collective-permute-start | bytes 786440 | tf_op jit(solution)/shard_map/ppermute | solution.py:22
  33.1 67.3 %collective-permute-start.2 = (f32[1,128,512]{2,1,0:T(8,128)S(1)}, f32[1,128,512]{2,1,0:T(8,128)S(1)}, u32[]{:S(2)}, u32[]{:S(2)}) collective-permute-start(f32[1,128,512]{2,1,0:T(8,128)S(1)} %collective-permute-done.1), channel_id=1, source_target_pairs={{0,1},{1,2},{2,3},{3,4},{4,5},{5,6},{6,7},{7,0},{8,9},{9,10},{10,1... | collective-permute-start | bytes 786440 | tf_op jit(solution)/shard_map/ppermute | solution.py:22
  35.2 126.5 %all-to-all-start = ((f32[8,128,128]{1,2,0:T(8,128)}), f32[8,128,128]{1,2,0:T(8,128)}, u32[]{:S(2)}, u32[]{:S(2)}) async-start(f32[8,128,128]{1,2,0:T(8,128)} %copy.9), calls=%async_computation | async-start | bytes 1048576 | tf_op jit(solution)/shard_map/all_to_all | solution.py:18
  41.2 114.2 %all-gather.3.cloned.1.call-start = ((), (), s32[]{:S(2)}) async-start(), calls=%async_computation.4 | async-start | bytes 1310720 | tf_op jit(solution)/shard_map/all_gather | solution.py:36
  100.3 59.2 %reduce-scatter.2.cloned.1.call-start = ((), (), s32[]{:S(2)}) async-start(), calls=%async_computation.3 | async-start | bytes 1310720 | tf_op jit(solution)/shard_map/reduce_scatter | solution.py:41
  100.3 12.2 %copy-start.1 = (f32[1024,1024]{1,0:T(8,128)S(1)}, f32[1024,1024]{1,0:T(8,128)}, u32[]{:S(2)}) copy-start(f32[1024,1024]{1,0:T(8,128)} %param.7) | copy-start | bytes 12582916
  100.4 10.7 %collective-permute-start.3 = (f32[1,128,512]{2,1,0:T(8,128)S(1)}, f32[1,128,512]{2,1,0:T(8,128)S(1)}, u32[]{:S(2)}, u32[]{:S(2)}) collective-permute-start(f32[1,128,512]{2,1,0:T(8,128)S(1)} %collective-permute-done.2), channel_id=1, source_target_pairs={{0,1},{1,2},{2,3},{3,4},{4,5},{5,6},{6,7},{7,0},{8,9},{9,10},{10,1... | collective-permute-start | bytes 786440 | tf_op jit(solution)/shard_map/ppermute | solution.py:22
  111.0 9.7 %copy-start.6 = (f32[1,128,512]{2,1,0:T(8,128)}, f32[1,128,512]{2,1,0:T(8,128)S(1)}, u32[]{:S(2)}) copy-start(f32[1,128,512]{2,1,0:T(8,128)S(1)} %collective-permute-done.3) | copy-start | bytes 786436
  111.0 9.7 %collective-permute-start.4 = (f32[1,128,512]{2,1,0:T(8,128)S(1)}, f32[1,128,512]{2,1,0:T(8,128)}, u32[]{:S(2)}, u32[]{:S(2)}) collective-permute-start(f32[1,128,512]{2,1,0:T(8,128)S(1)} %collective-permute-done.3), channel_id=1, source_target_pairs={{0,1},{1,2},{2,3},{3,4},{4,5},{5,6},{6,7},{7,0},{8,9},{9,10},{10,1... | collective-permute-start | bytes 786440 | tf_op jit(solution)/shard_map/ppermute | solution.py:22
  120.7 9.4 %collective-permute-start.5 = (f32[1,128,512]{2,1,0:T(8,128)}, f32[1,128,512]{2,1,0:T(8,128)}, u32[]{:S(2)}, u32[]{:S(2)}) collective-permute-start(f32[1,128,512]{2,1,0:T(8,128)} %collective-permute-done.4), channel_id=1, source_target_pairs={{0,1},{1,2},{2,3},{3,4},{4,5},{5,6},{6,7},{7,0},{8,9},{9,10},{10,1... | collective-permute-start | bytes 786440 | tf_op jit(solution)/shard_map/ppermute | solution.py:22
  123.4 6.8 %copy-start.3 = (f32[4,128,128]{1,2,0:T(8,128)}, f32[4,128,128]{1,2,0:T(8,128)S(1)}, u32[]{:S(2)}) copy-start(f32[4,128,128]{1,2,0:T(8,128)S(1)} %bitcast_multiply_fusion) | copy-start | bytes 786436
  123.4 21.2 %copy-start.7 = (f32[1,128,512]{2,1,0:T(8,128)S(1)}, f32[1,128,512]{2,1,0:T(8,128)}, u32[]{:S(2)}) copy-start(f32[1,128,512]{2,1,0:T(8,128)} %copy-done.6) | copy-start | bytes 786436
  130.2 9.4 %collective-permute-start.6 = (f32[1,128,512]{2,1,0:T(8,128)}, f32[1,128,512]{2,1,0:T(8,128)}, u32[]{:S(2)}, u32[]{:S(2)}) collective-permute-start(f32[1,128,512]{2,1,0:T(8,128)} %collective-permute-done.5), channel_id=1, source_target_pairs={{0,1},{1,2},{2,3},{3,4},{4,5},{5,6},{6,7},{7,0},{8,9},{9,10},{10,1... | collective-permute-start | bytes 786440 | tf_op jit(solution)/shard_map/ppermute | solution.py:22
  148.2 13.1 %copy-start.8 = (f32[1,128,128]{2,1,0:T(8,128)S(1)}, f32[1,128,128]{2,1,0:T(8,128)}, u32[]{:S(2)}) copy-start(f32[1,128,128]{2,1,0:T(8,128)} %param.10) | copy-start | bytes 196612
  161.3 3.8 %copy-start.4 = (f32[1024,128]{1,0:T(8,128)S(1)}, f32[1024,128]{1,0:T(8,128)}, u32[]{:S(2)}) copy-start(f32[1024,128]{1,0:T(8,128)} %param.8) | copy-start | bytes 1572868
  161.7 3.4 %copy-start.2 = (f32[1024,512]{1,0:T(8,128)S(1)}, f32[1024,512]{1,0:T(8,128)}, u32[]{:S(2)}) copy-start(f32[1024,512]{1,0:T(8,128)} %fusion.17) | copy-start | bytes 6291460
Sparse Core Ops, SparseCore 0:
  25.3 74.9 all-reduce.1
  101.8 16.0 all-gather.2
  133.3 26.1 reduce-scatter.1
